TPU v7x, 16 devices: a whole 2x2x2 slice. The times are simulated.
16 devices in a mesh: dp: 2 (over z), emb: 8 (over y, x, core).
Axes of the slice: x: 2, y: 2, z: 2, core: 2. Of those that a mesh axis runs over, the one named last changes fastest.
Arguments:
- token_ids: int32 [65536], P(('dp', 'emb'))
- x_init: bfloat16 [65536, 768], P(('dp', 'emb'))
- d_out: bfloat16 [65536, 768], P(('dp', 'emb'))
- tables: bfloat16 [4, 50304, 768], P(None, 'emb')
- w_up: bfloat16 [4, 768, 3072], replicated
- w_down: bfloat16 [4, 3072, 768], replicated
- w_gate: bfloat16 [4, 768, 768], replicated
- w_proj: bfloat16 [4, 768, 768], replicated
Outputs:
- output 1: bfloat16 [65536, 768], P(('dp', 'emb'))
- output 2: float32 [4, 50304, 768], P(None, 'emb')
All inputs are finite; a program needn't handle non-finite values.
Results may differ from a plain program's by a relative error of at most 0.0111161.
Values are sent between devices in bfloat16 or wider.
A program may use at most 1 GiB of HBM per device.

v0:
```python
import jax
import jax.numpy as jnp
from jax import lax
from jax.sharding import PartitionSpec as P

NORM_EPS = 1e-6


def rms_scale(x_f32):
    return lax.rsqrt(jnp.mean(x_f32 * x_f32, axis=-1, keepdims=True) + NORM_EPS)


def gelu_back(pre_act, grad_out):
    _, pull_back = jax.vjp(jax.nn.gelu, pre_act)
    return pull_back(grad_out)[0]


def layer_forward(x_in, emb_rows, w_up, w_down, w_gate, w_proj):
    x_f32 = x_in.astype(jnp.float32)
    normed = (x_f32 * rms_scale(x_f32)).astype(jnp.bfloat16)
    hidden = jax.nn.gelu(jnp.dot(normed, w_up, preferred_element_type=jnp.float32)).astype(jnp.bfloat16)
    gate_val = jax.nn.gelu(jnp.dot(normed, w_gate, preferred_element_type=jnp.float32)).astype(jnp.bfloat16)
    mixed_rows = (gate_val.astype(jnp.float32) * emb_rows.astype(jnp.float32)).astype(jnp.bfloat16)
    new_x = x_f32 + jnp.dot(hidden, w_down, preferred_element_type=jnp.float32) + jnp.dot(mixed_rows, w_proj, preferred_element_type=jnp.float32)
    return new_x.astype(jnp.bfloat16)


def table_grad(d_next, x_in, w_gate, w_proj):
    x_f32 = x_in.astype(jnp.float32)
    row_scale = rms_scale(x_f32)
    normed = x_f32 * row_scale
    norm_bf = normed.astype(jnp.bfloat16)
    pre_gate = jnp.dot(norm_bf, w_gate, preferred_element_type=jnp.float32)
    gate_val = jax.nn.gelu(pre_gate).astype(jnp.bfloat16)
    d_mixed = jnp.einsum('td,ed->te', d_next, w_proj, preferred_element_type=jnp.float32).astype(jnp.bfloat16)
    grad_rows = gate_val.astype(jnp.float32) * d_mixed.astype(jnp.float32)
    return grad_rows, (row_scale, normed, norm_bf, pre_gate, d_mixed)


def layer_backward(d_next, x_in, emb_rows, w_up, w_down, w_gate, w_proj):
    grad_rows, (row_scale, normed, norm_bf, pre_gate, d_mixed) = table_grad(d_next, x_in, w_gate, w_proj)
    d_emb = (d_mixed.astype(jnp.float32) * emb_rows.astype(jnp.float32)).astype(jnp.bfloat16)
    d_gate = gelu_back(pre_gate, d_emb.astype(jnp.float32)).astype(jnp.bfloat16)
    pre_up = jnp.dot(norm_bf, w_up, preferred_element_type=jnp.float32)
    d_hidden = jnp.einsum('td,fd->tf', d_next, w_down, preferred_element_type=jnp.float32).astype(jnp.bfloat16)
    d_up = gelu_back(pre_up, d_hidden.astype(jnp.float32)).astype(jnp.bfloat16)
    d_normed = jnp.einsum('tf,df->td', d_up, w_up, preferred_element_type=jnp.float32) + jnp.einsum('te,de->td', d_gate, w_gate, preferred_element_type=jnp.float32)
    d_resid = row_scale * (d_normed - normed * jnp.mean(d_normed * normed, axis=-1, keepdims=True))
    return (d_next.astype(jnp.float32) + d_resid).astype(jnp.bfloat16), grad_rows


def solution(mesh):
    emb_size = mesh.shape['emb']
    tok_spec = P(('dp', 'emb'))
    row_spec = P(('dp', 'emb'), None)
    tab_spec = P(None, 'emb', None)
    full_spec = P()

    def device_body(ids_loc, x_loc, dy_loc, tab_loc, w_up, w_down, w_gate, w_proj):
        tok_dev = ids_loc.shape[0]
        n_layers = tab_loc.shape[0]
        rows_dev = tab_loc.shape[1]
        cap_rows = 2 * tok_dev // emb_size
        send_size = emb_size * cap_rows
        id_owner = ids_loc // rows_dev
        row_offset = ids_loc - id_owner * rows_dev
        one_hot = (id_owner[:, None] == jnp.arange(emb_size, dtype=jnp.int32)[None, :]).astype(jnp.int32)
        tok_rank = jnp.sum((jnp.cumsum(one_hot, axis=0) - one_hot) * one_hot, axis=1)
        send_slot = id_owner * cap_rows + tok_rank
        src_tok = jnp.zeros((send_size,), jnp.int32).at[send_slot].set(jnp.arange(tok_dev, dtype=jnp.int32))
        used_mask = jnp.zeros((send_size,), jnp.float32).at[send_slot].set(1.0)
        send_off = jnp.zeros((send_size,), jnp.int32).at[send_slot].set(row_offset)
        recv_off = lax.all_to_all(send_off, 'emb', 0, 0, tiled=True)
        all_off = lax.all_gather(recv_off, 'dp', axis=0, tiled=True)

        x_cur = x_loc
        saved_acts = []
        for layer_idx in range(n_layers):
            served = jnp.take(tab_loc[layer_idx], recv_off, axis=0)
            returned = lax.all_to_all(served, 'emb', 0, 0, tiled=True)
            emb_rows = jnp.take(returned, send_slot, axis=0)
            saved_acts.append((x_cur, emb_rows))
            x_cur = layer_forward(x_cur, emb_rows, w_up[layer_idx], w_down[layer_idx], w_gate[layer_idx], w_proj[layer_idx])

        d_cur = dy_loc
        grad_tabs = [None] * n_layers
        for layer_idx in range(n_layers - 1, -1, -1):
            x_in, emb_rows = saved_acts[layer_idx]
            if layer_idx > 0:
                d_cur, grad_rows = layer_backward(d_cur, x_in, emb_rows, w_up[layer_idx], w_down[layer_idx], w_gate[layer_idx], w_proj[layer_idx])
            else:
                grad_rows = table_grad(d_cur, x_in, w_gate[0], w_proj[0])[0]
            send_grad = jnp.take(grad_rows, src_tok, axis=0) * used_mask[:, None]
            got_grad = lax.all_to_all(send_grad, 'emb', 0, 0, tiled=True)
            all_grad = lax.all_gather(got_grad, 'dp', axis=0, tiled=True)
            grad_tabs[layer_idx] = jax.ops.segment_sum(all_grad, all_off, num_segments=rows_dev)
        return x_cur, jnp.stack(grad_tabs)

    return jax.shard_map(device_body, mesh=mesh, in_specs=(tok_spec, row_spec, row_spec, tab_spec, full_spec, full_spec, full_spec, full_spec), out_specs=(row_spec, tab_spec), check_vma=False)
```

profile of v0, /device:TPU:0, one launch (start us, length us, event | category | flops | bytes accessed | tf_op | source)
XLA Modules:
  0.0 4273.0 jit_solution(3094327714587375569)
XLA Ops:
  60.8 42.0 gather_fusion
  102.8 42.2 gather_fusion.2
  145.1 42.2 gather_fusion.4
  187.2 42.3 gather_fusion.6
  880.3 54.5 %fusion.147.clone.5 = bf16[4096,3072]{1,0:T(8,128)(2,1)} fusion(f32[4096,3072]{1,0:T(8,128)} %fusion.183, bf16[4096,768]{1,0:T(8,128)(2,1)S(1)} %bitcast.224, bf16[4,3072,768]{2,1,0:T(8,128)(2,1)} %param.19), kind=kOutput, calls=%fused_computation.35.clone.clone.clone.clone.clone.clone.2 | convolution fusion | flops 19604176896 | bytes 86507520 | tf_op jit(solution)/shard_map/td,fd->tf/dot_general | solution.py:45
  1007.9 58.8 %fusion.150.clone.5 = bf16[4096,3072]{1,0:T(8,128)(2,1)} fusion(f32[4096,3072]{1,0:T(8,128)} %fusion.187, bf16[4096,768]{0,1:T(8,128)(2,1)S(1)} %fusion.90, bf16[4,3072,768]{2,1,0:T(8,128)(2,1)} %param.19), kind=kOutput, calls=%fused_computation.40.clone.clone.clone.clone.clone.clone.2 | convolution fusion | flops 19604176896 | bytes 86507520 | tf_op jit(solution)/shard_map/td,fd->tf/dot_general | solution.py:45
  1141.3 59.0 %fusion.153.clone.5 = bf16[4096,3072]{1,0:T(8,128)(2,1)} fusion(f32[4096,3072]{1,0:T(8,128)} %fusion.191, bf16[4096,768]{0,1:T(8,128)(2,1)S(1)} %fusion.95, bf16[4,3072,768]{2,1,0:T(8,128)(2,1)} %param.19), kind=kOutput, calls=%fused_computation.45.clone.clone.clone.clone.clone.clone.2 | convolution fusion | flops 19604176896 | bytes 86507520 | tf_op jit(solution)/shard_map/td,fd->tf/dot_general | solution.py:45
  1265.9 43.6 %gather_fusion.8 = f32[8192,768]{1,0:T(8,128)} fusion(f32[4096,768]{1,0:T(8,128)} %convert_multiply_fusion.29, s32[8192]{0:T(1024)S(1)} %copy-done.5), kind=kCustom, calls=%fused_computation.2.clone | custom fusion | bytes 50364416 | tf_op jit(solution)/shard_map/jit(_take)/gather | solution.py:93
  1309.5 44.0 %gather_fusion.9 = f32[8192,768]{1,0:T(8,128)} fusion(f32[4096,768]{1,0:T(8,128)} %get-tuple-element.40, s32[8192]{0:T(1024)S(1)} %copy-done.5), kind=kCustom, calls=%fused_computation.9.clone | custom fusion | bytes 50364416 | tf_op jit(solution)/shard_map/jit(_take)/gather | solution.py:93
  1353.5 44.1 %gather_fusion.10 = f32[8192,768]{1,0:T(8,128)} fusion(f32[4096,768]{1,0:T(8,128)} %get-tuple-element.42, s32[8192]{0:T(1024)S(1)} %copy-done.5), kind=kCustom, calls=%fused_computation.10.clone | custom fusion | bytes 50364416 | tf_op jit(solution)/shard_map/jit(_take)/gather | solution.py:93
  1397.6 44.0 %gather_fusion.11 = f32[8192,768]{1,0:T(8,128)} fusion(f32[4096,768]{1,0:T(8,128)} %get-tuple-element.44, s32[8192]{0:T(1024)S(1)} %copy-done.5), kind=kCustom, calls=%fused_computation.11.clone | custom fusion | bytes 50364416 | tf_op jit(solution)/shard_map/jit(_take)/gather | solution.py:93
  1441.6 67.1 %select_multiply_fusion.3 = (f32[8192,768]{1,0:T(8,128)}, f32[8192,768]{1,0:T(8,128)}, f32[8192,768]{1,0:T(8,128)}, f32[8192,768]{1,0:T(8,128)}) fusion(f32[8192,768]{1,0:T(8,128)} %gather_fusion.8, f32[8192]{0:T(1024)S(1)} %copy-done.10, pred[8192]{0:T(1024)(128)(4,1)S(1)} %copy-done.17, f32[8192,768]{1,0:T(8,128)} %gather_fusion.9, ...), kind=kLoop, calls=%fused_computation.77 | loop fusion | flops 50331648 | bytes 201367552 | tf_op jit(solution)/shard_map/mul | solution.py:93
  1508.7 282.8 %all_to_all.108 = f32[8,1024,768]{2,1,0:T(8,128)} all-to-all(f32[8,1024,768]{2,1,0:T(8,128)} %bitcast.212), channel_id=1, replica_groups=mesh['dp'=2,'emb'=8] {'emb'}, dimensions={0} | all-to-all | bytes 50331648 | tf_op jit(solution)/shard_map/all_to_all | solution.py:94
  1791.6 282.8 %all_to_all.109 = f32[8,1024,768]{2,1,0:T(8,128)} all-to-all(f32[8,1024,768]{2,1,0:T(8,128)} %bitcast.211), channel_id=1, replica_groups=mesh['dp'=2,'emb'=8] {'emb'}, dimensions={0} | all-to-all | bytes 50331648 | tf_op jit(solution)/shard_map/all_to_all | solution.py:94
  2074.4 282.8 %all_to_all.110 = f32[8,1024,768]{2,1,0:T(8,128)} all-to-all(f32[8,1024,768]{2,1,0:T(8,128)} %bitcast.210), channel_id=1, replica_groups=mesh['dp'=2,'emb'=8] {'emb'}, dimensions={0} | all-to-all | bytes 50331648 | tf_op jit(solution)/shard_map/all_to_all | solution.py:94
  2357.3 282.8 %all_to_all.111 = f32[8,1024,768]{2,1,0:T(8,128)} all-to-all(f32[8,1024,768]{2,1,0:T(8,128)} %bitcast.209), channel_id=1, replica_groups=mesh['dp'=2,'emb'=8] {'emb'}, dimensions={0} | all-to-all | bytes 50331648 | tf_op jit(solution)/shard_map/all_to_all | solution.py:94
  2705.0 118.8 %scatter_custom_fusion.6 = f32[6288,768]{1,0:T(8,128)} fusion(s32[16384]{0:T(1024)S(1)} %all_gather.15, f32[16384,768]{1,0:T(8,128)} %all-gather.11.cloned.1.call-done, f32[]{:T(128)} %constant.41.clone.1), kind=kCustom, calls=%fused_computation.213 | custom fusion | flops 12582912 | bytes 19317248 | tf_op jit(solution)/shard_map/scatter-add | solution.py:96
  2823.8 119.8 %all-gather.9.cloned.1.call-done = f32[16384,768]{1,0:T(8,128)} async-done(((f32[8192,768]{1,0:T(8,128)}), f32[16384,768]{1,0:T(8,128)}) %all-gather.9.cloned.1.call-update) | async-done | bytes 50331664 | tf_op jit(solution)/shard_map/all_gather | solution.py:95
  2943.6 118.6 %scatter_custom_fusion.5 = f32[6288,768]{1,0:T(8,128)} fusion(s32[16384]{0:T(1024)S(1)} %all_gather.15, f32[16384,768]{1,0:T(8,128)} %all-gather.9.cloned.1.call-done, f32[]{:T(128)} %constant.41.clone.1), kind=kCustom, calls=%fused_computation.215 | custom fusion | flops 12582912 | bytes 19317248 | tf_op jit(solution)/shard_map/scatter-add | solution.py:96
  3062.2 458.2 %all-gather.7.cloned.1.call-done = f32[16384,768]{1,0:T(8,128)} async-done(((f32[8192,768]{1,0:T(8,128)}), f32[16384,768]{1,0:T(8,128)}) %all-gather.7.cloned.1.call-update) | async-done | bytes 50331664 | tf_op jit(solution)/shard_map/all_gather | solution.py:95
  3520.4 118.8 %scatter_custom_fusion.4 = f32[6288,768]{1,0:T(8,128)} fusion(s32[16384]{0:T(1024)S(1)} %all_gather.15, f32[16384,768]{1,0:T(8,128)} %all-gather.7.cloned.1.call-done, f32[]{:T(128)} %constant.41.clone.1), kind=kCustom, calls=%fused_computation.217 | custom fusion | flops 12582912 | bytes 19317248 | tf_op jit(solution)/shard_map/scatter-add | solution.py:96
  3639.2 457.9 %all-gather.5.cloned.1.call-done = f32[16384,768]{1,0:T(8,128)} async-done(((f32[8192,768]{1,0:T(8,128)}), f32[16384,768]{1,0:T(8,128)}) %all-gather.5.cloned.1.call-update) | async-done | bytes 50331664 | tf_op jit(solution)/shard_map/all_gather | solution.py:95
  4097.1 118.7 %scatter_custom_fusion.3 = f32[6288,768]{1,0:T(8,128)} fusion(s32[16384]{0:T(1024)S(1)} %all_gather.15, f32[16384,768]{1,0:T(8,128)} %all-gather.5.cloned.1.call-done, f32[]{:T(128)} %constant.41.clone.1), kind=kCustom, calls=%fused_computation.219 | custom fusion | flops 12582912 | bytes 19317248 | tf_op jit(solution)/shard_map/scatter-add | solution.py:96
  4215.8 50.3 %pad_maximum_fusion = f32[4,6288,768]{2,1,0:T(8,128)} fusion(f32[1,6288,768]{2,1,0:T(8,128)} %bitcast.213, f32[1,6288,768]{2,1,0:T(8,128)} %bitcast.214, f32[1,6288,768]{2,1,0:T(8,128)} %bitcast.215, f32[1,6288,768]{2,1,0:T(8,128)} %bitcast.216), kind=kLoop, calls=%fused_computation.19 | loop fusion | flops 57950208 | bytes 154533888 | tf_op jit(solution)/shard_map/stack | solution.py:97
  (139 shorter events, 982.4 us)
Async XLA Ops:
  12.3 48.4 %copy-start.15 = (s32[4096]{0:T(1024)}, s32[4096]{0:T(1024)S(1)}, u32[]{:S(2)}) copy-start(s32[4096]{0:T(1024)S(1)} %get-tuple-element.12) | copy-start | bytes 49156
  28.4 32.4 all-to-all-start
  60.8 42.1 copy-start.6
  261.1 144.5 %all-to-all-start.1 = ((bf16[8,1024,768]{2,1,0:T(8,128)(2,1)}), bf16[8,1024,768]{2,1,0:T(8,128)(2,1)}, u32[]{:S(2)}, u32[]{:S(2)}) async-start(bf16[8,1024,768]{2,1,0:T(8,128)(2,1)} %bitcast.220), calls=%async_computation.1 | async-start | bytes 25165824 | tf_op jit(solution)/shard_map/all_to_all | solution.py:80
  405.6 144.7 %all-to-all-start.2 = ((bf16[8,1024,768]{2,1,0:T(8,128)(2,1)}), bf16[8,1024,768]{2,1,0:T(8,128)(2,1)}, u32[]{:S(2)}, u32[]{:S(2)}) async-start(bf16[8,1024,768]{2,1,0:T(8,128)(2,1)} %bitcast.219), calls=%async_computation.2 | async-start | bytes 25165824 | tf_op jit(solution)/shard_map/all_to_all | solution.py:80
  411.4 25.4 copy-start.18
  550.4 144.6 %all-to-all-start.3 = ((bf16[8,1024,768]{2,1,0:T(8,128)(2,1)}), bf16[8,1024,768]{2,1,0:T(8,128)(2,1)}, u32[]{:S(2)}, u32[]{:S(2)}) async-start(bf16[8,1024,768]{2,1,0:T(8,128)(2,1)} %bitcast.218), calls=%async_computation.3 | async-start | bytes 25165824 | tf_op jit(solution)/shard_map/all_to_all | solution.py:80
  695.0 144.3 %all-to-all-start.4 = ((bf16[8,1024,768]{2,1,0:T(8,128)(2,1)}), bf16[8,1024,768]{2,1,0:T(8,128)(2,1)}, u32[]{:S(2)}, u32[]{:S(2)}) async-start(bf16[8,1024,768]{2,1,0:T(8,128)(2,1)} %bitcast.217), calls=%async_computation.4 | async-start | bytes 25165824 | tf_op jit(solution)/shard_map/all_to_all | solution.py:80
  700.3 2004.7 %all-gather.11.cloned.1.call-start = ((), (), s32[]{:S(2)}) async-start(), calls=%async_computation.12 | async-start | bytes 75497472 | tf_op jit(solution)/shard_map/all_gather | solution.py:95
  839.3 41.0 slice-start.2
  880.3 54.5 %copy-start.19 = (pred[4096]{0:T(1024)(128)(4,1)S(1)}, pred[4096]{0:T(1024)(128)(4,1)}, u32[]{:S(2)}) copy-start(pred[4096]{0:T(1024)(128)(4,1)} %get-tuple-element.11) | copy-start | bytes 12292
  934.9 20.1 copy-start.3
  934.9 20.1 copy-start.14
  934.9 47.6 %slice-start = ((s8[6291456]{0:T(1024)(128)(4,1)}), s8[4194304]{0:T(1024)(128)(4,1)S(1)}, s32[]{:S(2)}) async-start(s8[6291456]{0:T(1024)(128)(4,1)} %bitcast.221), calls=%async_computation.13 | async-start | bytes 8388608
  954.9 27.5 slice-start.1
  1007.9 58.8 %copy-start.20 = (pred[4096]{0:T(1024)(128)(4,1)S(1)}, pred[4096]{0:T(1024)(128)(4,1)}, u32[]{:S(2)}) copy-start(pred[4096]{0:T(1024)(128)(4,1)} %get-tuple-element.11) | copy-start | bytes 12292
  1066.7 20.3 copy-start.4
  1066.7 20.3 copy-start.12
  1141.3 59.0 %copy-start.21 = (pred[4096]{0:T(1024)(128)(4,1)S(1)}, pred[4096]{0:T(1024)(128)(4,1)}, u32[]{:S(2)}) copy-start(pred[4096]{0:T(1024)(128)(4,1)} %get-tuple-element.11) | copy-start | bytes 12292
  1397.6 44.0 %copy-start.10 = (f32[8192]{0:T(1024)S(1)}, f32[8192]{0:T(1024)}, u32[]{:S(2)}) copy-start(f32[8192]{0:T(1024)} %scatter_custom_fusion.2) | copy-start | bytes 98308
  1397.6 44.0 %copy-start.17 = (pred[8192]{0:T(1024)(128)(4,1)S(1)}, pred[8192]{0:T(1024)(128)(4,1)}, u32[]{:S(2)}) copy-start(pred[8192]{0:T(1024)(128)(4,1)} %compare_and_fusion) | copy-start | bytes 24580
  1791.5 1152.1 %all-gather.9.cloned.1.call-start = ((), (), s32[]{:S(2)}) async-start(), calls=%async_computation.11 | async-start | bytes 75497472 | tf_op jit(solution)/shard_map/all_gather | solution.py:95
  2074.4 1446.0 %all-gather.7.cloned.1.call-start = ((), (), s32[]{:S(2)}) async-start(), calls=%async_computation.10 | async-start | bytes 75497472 | tf_op jit(solution)/shard_map/all_gather | solution.py:95
  2357.3 1739.8 %all-gather.5.cloned.1.call-start = ((), (), s32[]{:S(2)}) async-start(), calls=%async_computation.9 | async-start | bytes 75497472 | tf_op jit(solution)/shard_map/all_gather | solution.py:95
  (12 other events, 164.1 us)
Sparse Core Ops, SparseCore 0:
  1791.6 574.4 all-gather.10
  2367.6 575.9 all-gather.8
  2945.1 575.2 all-gather.6
  3521.8 575.2 all-gather.4
where the time goes:
time: 4280 us; the launch traced here: 4270 us
  waiting for transfers between devices  1150 us (27%)
  blocking collectives  1140 us (27%)
  matrix products  748 us (17%)
  other arithmetic  652 us (15%)
  local copies, waits for them, and re-layouts  548 us (13%)
    all_to_all x4, blocking collectives, device_body(): got_grad = lax.all_to_all(send_grad, 'emb', 0, 0, tiled=True)  1130 us
    all_gather x4, waiting for transfers between devices, device_body(): all_grad = lax.all_gather(got_grad, 'dp', axis=0, tiled=True)  1040 us
    scatter-add x4, other arithmetic, device_body(): jax.ops.segment_sum(all_grad, all_off, num_segments=rows_dev)  475 us
    gather x4, local copies, waits for them, and re-layouts, device_body(): send_grad = jnp.take(grad_rows, src_tok, axis=0) * used_mask[:, None]  176 us
    dot_general x3, matrix products, layer_backward(): jnp.einsum('td,fd->tf', d_next, w_down, preferred_element_type=jnp.float32)  172 us
    gather x4, local copies, waits for them, and re-layouts, device_body(): served = jnp.take(tab_loc[layer_idx], recv_off, axis=0)  169 us
    dot_general x4, matrix products, layer_forward(): jnp.dot(hidden, w_down, preferred_element_type=jnp.float32)  137 us
    dot_general x4, matrix products, layer_forward(): jnp.dot(normed, w_up, preferred_element_type=jnp.float32)  128 us
  transfers between devices with their start and end apart: 9, of which 7 were waited for; matrix products, arithmetic and copies ran while one was open for 21% of the time, Pallas kernels for 0%

commit v1 on v0

v1 whole, which is shorter than its diff:
```python
import functools

import jax
import jax.numpy as jnp
from jax import lax
from jax.experimental import pallas as pl
from jax.experimental.pallas import tpu as pltpu
from jax.sharding import PartitionSpec as P

NORM_EPS = 1e-6
GELU_K = 0.7978845608028654
GELU_C = 0.044715
DEAD = 1 << 30
TILE = 512
HALF = 256
LAG = 1
SEG_TILE = 256
ROWS = 256
CHUNKS = 4
VMEM = 66_000_000
BF = jnp.bfloat16
F32 = jnp.float32


def dot(a, b):
    return lax.dot_general(a, b, (((1,), (0,)), ((), ())), preferred_element_type=F32)


def dot_t(a, b):
    return lax.dot_general(a, b, (((1,), (1,)), ((), ())), preferred_element_type=F32)


def gelu_both(p):
    sq = p * p
    half = 0.5 * jnp.tanh(p * (GELU_K + (GELU_K * GELU_C) * sq))
    cdf = 0.5 + half
    value = p * cdf
    slope = (0.5 - half) * (2.0 * GELU_K + (6.0 * GELU_K * GELU_C) * sq)
    return value, cdf + value * slope


def weave(streams):
    waiting = [LAG * k for k in range(len(streams))]
    alive = list(streams)
    while alive:
        for k, stream in enumerate(streams):
            if stream not in alive:
                continue
            if waiting[k] > 0:
                waiting[k] -= 1
            elif next(stream, None) is None:
                alive.remove(stream)


def forward_kernel(last, nt_ref, x_ref, e_ref, wu_ref, wd_ref, wg_ref, wp_ref, *rest):
    pl.when(pl.program_id(1) < nt_ref[0])(lambda: forward_tile(last, x_ref, e_ref, wu_ref, wd_ref, wg_ref, wp_ref, *rest))


def forward_tile(last, x_ref, e_ref, wu_ref, wd_ref, wg_ref, wp_ref, *rest):
    if last:
        xl_ref, du_ref, dg_ref, a_ref, out_ref, x_scr, sem = rest
    else:
        xl_ref, du_ref, dg_ref, a_ref, x_scr, sem = rest
    layer, tile = pl.program_id(0), pl.program_id(1)
    size = xl_ref.shape[1]

    @pl.when(jnp.logical_and(layer == 0, tile == 0))
    def _():
        copy = pltpu.make_async_copy(x_ref, x_scr, sem)
        copy.start()
        copy.wait()

    ff = wu_ref.shape[2]
    step = ff // CHUNKS
    cols = [slice(c * step, (c + 1) * step) for c in range(CHUNKS)]

    def stream(k, down):
        part = slice(k * HALF, (k + 1) * HALF)
        rows = pl.ds(pl.multiple_of(tile * size + k * HALF, HALF), HALF)
        x_bf = x_scr[rows, :]
        xl_ref[0, part, :] = x_bf
        x = x_bf.astype(F32)
        r = lax.rsqrt(jnp.mean(x * x, axis=-1, keepdims=True) + NORM_EPS)
        u = (x * r).astype(BF)
        pre_gate = dot(u, wg_ref[0])
        now = dot(u, wu_ref[0, :, cols[0]])
        yield True
        gate, d_gate = gelu_both(pre_gate)
        a = gate.astype(BF)
        a_ref[0, part, :] = a
        dg_ref[0, part, :] = d_gate
        acc = None
        for c in range(CHUNKS):
            if c + 1 < CHUNKS:
                later = dot(u, wu_ref[0, :, cols[c + 1]])
            h, d_up = gelu_both(now)
            du_ref[0, part, cols[c]] = d_up
            if down:
                if c == 0:
                    s = (a.astype(F32) * e_ref[0, part, :].astype(F32)).astype(BF)
                    acc = x + dot(s, wp_ref[0])
                acc = acc + dot(h.astype(BF), wd_ref[0, cols[c], :])
            if c + 1 < CHUNKS:
                now = later
            yield True
        if down:
            x_new = acc.astype(BF)
            x_scr[rows, :] = x_new
            if last:
                out_ref[part, :] = x_new

    def run(down):
        weave([stream(k, down) for k in range(size // HALF)])

    if last:
        run(True)
    else:
        is_last = layer == pl.num_programs(0) - 1
        pl.when(jnp.logical_not(is_last))(lambda: run(True))
        pl.when(is_last)(lambda: run(False))


def backward_kernel(nt_ref, n_ref, *refs):
    pl.when(pl.program_id(1) < nt_ref[0])(lambda: backward_tile(n_ref, *refs))


def backward_tile(n_ref, d_ref, xl_ref, du_ref, dg_ref, a_ref, e_ref, wu_ref, wd_ref, wg_ref, wp_ref, hi_ref, lo_ref, c_scr, sem):
    step_id, tile = pl.program_id(0), pl.program_id(1)
    size = xl_ref.shape[1]

    @pl.when(jnp.logical_and(step_id == 0, tile == 0))
    def _():
        copy = pltpu.make_async_copy(d_ref, c_scr, sem)
        copy.start()
        copy.wait()

    ff = wu_ref.shape[2]
    step = ff // CHUNKS
    cols = [slice(c * step, (c + 1) * step) for c in range(CHUNKS)]

    def stream(k, down):
        part = slice(k * HALF, (k + 1) * HALF)
        rows = pl.ds(pl.multiple_of(tile * size + k * HALF, HALF), HALF)
        c = c_scr[rows, :]
        ds = dot_t(c, wp_ref[0]).astype(BF)
        if down:
            now = dot_t(c, wd_ref[0, cols[0], :])
            later = dot_t(c, wd_ref[0, cols[1], :])
        yield True
        ds_f = ds.astype(F32)
        live = tile * size + k * HALF + lax.broadcasted_iota(jnp.int32, ds_f.shape, 0) < n_ref[0]
        grad = jnp.where(live, a_ref[0, part, :].astype(F32) * ds_f, 0.0)
        hi = grad.astype(BF)
        hi_ref[0, part, :] = hi
        lo_ref[0, part, :] = (grad - hi.astype(F32)).astype(BF)
        if down:
            de = (ds_f * e_ref[0, part, :].astype(F32)).astype(BF)
            dgate = (dg_ref[0, part, :] * de.astype(F32)).astype(BF)
            yield True
            m = dot_t(dgate, wg_ref[0])
            for q in range(CHUNKS):
                dup = (du_ref[0, part, cols[q]] * now.astype(BF).astype(F32)).astype(BF)
                now = later
                if q + 2 < CHUNKS:
                    later = dot_t(c, wd_ref[0, cols[q + 2], :])
                m = m + dot_t(dup, wu_ref[0, :, cols[q]])
                yield True
            x = xl_ref[0, part, :].astype(F32)
            r = lax.rsqrt(jnp.mean(x * x, axis=-1, keepdims=True) + NORM_EPS)
            n = x * r
            corr = jnp.mean(m * n, axis=-1, keepdims=True)
            c_scr[rows, :] = (c.astype(F32) + r * (m - n * corr)).astype(BF)

    def run(down):
        weave([stream(k, down) for k in range(size // HALF)])

    bottom = step_id == pl.num_programs(0) - 1
    pl.when(jnp.logical_not(bottom))(lambda: run(True))
    pl.when(bottom)(lambda: run(False))


def run_forward(last, nt, x, e, w_up, w_down, w_gate, w_proj):
    n, dim = x.shape
    layers, _, ff = w_up.shape
    t = TILE

    def per_layer(l, i, nt_ref):
        return (l, 0, 0)

    def saved(l, i, nt_ref):
        return (jnp.maximum(l - 1, 0), jnp.minimum(i, nt_ref[0] - 1), 0)

    def tok(l, i, nt_ref):
        return (l, jnp.minimum(i, nt_ref[0] - 1), 0)

    outs = [
        (jax.ShapeDtypeStruct((layers - 1, n, dim), BF), pl.BlockSpec((1, t, dim), saved)),
        (jax.ShapeDtypeStruct((layers - 1, n, ff), F32), pl.BlockSpec((1, t, ff), saved)),
        (jax.ShapeDtypeStruct((layers - 1, n, dim), F32), pl.BlockSpec((1, t, dim), saved)),
        (jax.ShapeDtypeStruct((layers, n, dim), BF), pl.BlockSpec((1, t, dim), tok)),
    ]
    if last:
        outs.append((jax.ShapeDtypeStruct((n, dim), BF), pl.BlockSpec((t, dim), lambda l, i, nt_ref: (jnp.minimum(i, nt_ref[0] - 1), 0))))
    flops = layers * n * 2 * dim * (2 * ff + 2 * dim)
    return pl.pallas_call(
        functools.partial(forward_kernel, last),
        out_shape=[o[0] for o in outs],
        grid_spec=pltpu.PrefetchScalarGridSpec(
            num_scalar_prefetch=1, grid=(layers, n // t),
            in_specs=[pl.BlockSpec(memory_space=pl.ANY), pl.BlockSpec((1, t, dim), tok),
                      pl.BlockSpec((1, dim, ff), per_layer), pl.BlockSpec((1, ff, dim), per_layer),
                      pl.BlockSpec((1, dim, dim), per_layer), pl.BlockSpec((1, dim, dim), per_layer)],
            out_specs=[o[1] for o in outs],
            scratch_shapes=[pltpu.VMEM((n, dim), BF), pltpu.SemaphoreType.DMA]),
        compiler_params=pltpu.CompilerParams(dimension_semantics=("arbitrary", "arbitrary"), vmem_limit_bytes=VMEM),
        cost_estimate=pl.CostEstimate(flops=flops // 2, bytes_accessed=n * ff * 4 * layers, transcendentals=0),
        name="fwd",
    )(nt, x, e, w_up, w_down, w_gate, w_proj)


def run_backward(nt, n_live, d, xl, du, dg, a, e, w_up, w_down, w_gate, w_proj):
    n, dim = d.shape
    layers, _, ff = w_up.shape
    t = TILE
    top = layers - 1

    def per_layer(g, i, nt_ref, n_ref):
        return (top - g, 0, 0)

    def upper_layer(g, i, nt_ref, n_ref):
        return (jnp.maximum(top - g, 1), 0, 0)

    def saved(g, i, nt_ref, n_ref):
        return (jnp.maximum(top - 1 - g, 0), jnp.where(g == top, nt_ref[0] - 1, jnp.minimum(i, nt_ref[0] - 1)), 0)

    def tok(g, i, nt_ref, n_ref):
        return (top - g, jnp.minimum(i, nt_ref[0] - 1), 0)

    flops = layers * n * 2 * dim * (2 * ff + 2 * dim)
    return pl.pallas_call(
        backward_kernel,
        out_shape=[jax.ShapeDtypeStruct((layers, n, dim), BF)] * 2,
        grid_spec=pltpu.PrefetchScalarGridSpec(
            num_scalar_prefetch=2, grid=(layers, n // t),
            in_specs=[pl.BlockSpec(memory_space=pl.ANY), pl.BlockSpec((1, t, dim), saved),
                      pl.BlockSpec((1, t, ff), saved), pl.BlockSpec((1, t, dim), saved),
                      pl.BlockSpec((1, t, dim), tok), pl.BlockSpec((1, t, dim), tok),
                      pl.BlockSpec((1, dim, ff), upper_layer), pl.BlockSpec((1, ff, dim), upper_layer),
                      pl.BlockSpec((1, dim, dim), upper_layer), pl.BlockSpec((1, dim, dim), per_layer)],
            out_specs=[pl.BlockSpec((1, t, dim), tok)] * 2,
            scratch_shapes=[pltpu.VMEM((n, dim), BF), pltpu.SemaphoreType.DMA]),
        compiler_params=pltpu.CompilerParams(dimension_semantics=("arbitrary", "arbitrary"), vmem_limit_bytes=VMEM),
        cost_estimate=pl.CostEstimate(flops=flops // 2, bytes_accessed=n * ff * 4 * layers, transcendentals=0),
        name="bwd",
    )(nt, n_live, d, xl, du, dg, a, e, w_up, w_down, w_gate, w_proj)


def pick_kernel(rows_dev, num_ref, *refs):
    pl.when(pl.program_id(0) < num_ref[0])(lambda: pick_step(rows_dev, *refs))


def pick_step(rows_dev, tile_ref, blk_ref, off_ref, tab_ref, e_ref):
    p = pl.program_id(0)
    blk = blk_ref[p]
    layers, size = tab_ref.shape[0], tab_ref.shape[1]
    hot = (off_ref[0] - blk * size == lax.broadcasted_iota(jnp.int32, (size, off_ref.shape[2]), 0)).astype(F32)
    hot = hot.T.astype(BF)
    fresh = jnp.logical_or(p == 0, tile_ref[p] != tile_ref[jnp.maximum(p - 1, 0)])
    valid = rows_dev - blk * size
    tail = valid < size

    @pl.when(fresh)
    def _():
        e_ref[...] = jnp.zeros_like(e_ref)

    def work(clip):
        for l in range(layers):
            rows = tab_ref[l]
            if clip:
                keep = lax.broadcasted_iota(jnp.int32, rows.shape, 0) < valid
                rows = jnp.where(keep, rows.astype(F32), 0.0).astype(BF)
            e_ref[l] += dot(hot, rows).astype(BF)

    pl.when(tail)(lambda: work(True))
    pl.when(jnp.logical_not(tail))(lambda: work(False))


def run_pick(pairs, tile, blk, off, tables):
    layers, rows_dev, dim = tables.shape
    n = off.shape[0]
    t = SEG_TILE
    return pl.pallas_call(
        functools.partial(pick_kernel, rows_dev),
        out_shape=jax.ShapeDtypeStruct((layers, n, dim), BF),
        grid_spec=pltpu.PrefetchScalarGridSpec(
            num_scalar_prefetch=3, grid=(tile.shape[0],),
            in_specs=[pl.BlockSpec((1, 1, t), lambda p, nr, tr, br: (tr[p], 0, 0)),
                      pl.BlockSpec((layers, ROWS, dim), lambda p, nr, tr, br: (0, br[p], 0))],
            out_specs=pl.BlockSpec((layers, t, dim), lambda p, nr, tr, br: (0, tr[p], 0))),
        compiler_params=pltpu.CompilerParams(dimension_semantics=("arbitrary",), vmem_limit_bytes=VMEM),
        cost_estimate=pl.CostEstimate(flops=40_000_000_000, bytes_accessed=n * dim * 16, transcendentals=0),
        name="pick",
    )(pairs.reshape(1), tile, blk, off.reshape(n // t, 1, t), tables)


def sum_kernel(num_ref, *refs):
    pl.when(pl.program_id(0) < num_ref[0])(lambda: sum_step(*refs))


def sum_step(blk_ref, own_ref, dup_ref, sel_ref, pos_own, pos_dup, off_o, hi_o, lo_o, off_d, hi_d, lo_d, out_ref):
    s = pl.program_id(0)
    blk = blk_ref[s]
    layers, rows, dim = out_ref.shape
    t = off_o.shape[2]
    half = 128

    @pl.when(jnp.logical_or(s == 0, blk != blk_ref[jnp.maximum(s - 1, 0)]))
    def _():
        out_ref[...] = jnp.zeros_like(out_ref)

    def add(tile, pos, off_ref, hi_ref, lo_ref):
        first, end = pos[blk], pos[blk + 1]
        for j in range(t // half):
            at = tile * t + j * half

            @pl.when(jnp.logical_and(at < end, at + half > first))
            def _():
                cols = pl.ds(j * half, half)
                hot = (off_ref[0, :, cols] - blk * rows == lax.broadcasted_iota(jnp.int32, (rows, half), 0)).astype(F32).astype(BF)
                hot = jnp.concatenate([hot, hot], axis=1)
                for l in range(layers):
                    both = jnp.concatenate([hi_ref[l, cols, :], lo_ref[l, cols, :]], axis=0)
                    out_ref[l] += dot(hot, both)

    @pl.when(sel_ref[s] == 0)
    def _():
        add(own_ref[s], pos_own, off_o, hi_o, lo_o)

    @pl.when(sel_ref[s] == 1)
    def _():
        add(dup_ref[s], pos_dup, off_d, hi_d, lo_d)


def run_sum(rows_dev, steps, lists, off_own, hi_own, lo_own, off_dup, hi_dup, lo_dup):
    layers, n, dim = hi_own.shape
    t = SEG_TILE
    own = lambda s, m, b, o, d, se, po, pd: (0, o[s], 0)
    dup = lambda s, m, b, o, d, se, po, pd: (0, d[s], 0)
    own_off = lambda s, m, b, o, d, se, po, pd: (o[s], 0, 0)
    dup_off = lambda s, m, b, o, d, se, po, pd: (d[s], 0, 0)
    big = (layers, t, dim)
    return pl.pallas_call(
        sum_kernel,
        out_shape=jax.ShapeDtypeStruct((layers, rows_dev, dim), F32),
        grid_spec=pltpu.PrefetchScalarGridSpec(
            num_scalar_prefetch=7, grid=(lists[0].shape[0],),
            in_specs=[pl.BlockSpec((1, 1, t), own_off), pl.BlockSpec(big, own), pl.BlockSpec(big, own),
                      pl.BlockSpec((1, 1, t), dup_off), pl.BlockSpec(big, dup), pl.BlockSpec(big, dup)],
            out_specs=pl.BlockSpec((layers, ROWS, dim), lambda s, m, b, o, d, se, po, pd: (0, b[s], 0))),
        compiler_params=pltpu.CompilerParams(dimension_semantics=("arbitrary",), vmem_limit_bytes=VMEM),
        cost_estimate=pl.CostEstimate(flops=60_000_000_000, bytes_accessed=layers * dim * 4 * (2 * n + rows_dev), transcendentals=0),
        name="tabsum",
    )(steps.reshape(1), *lists, off_own.reshape(n // t, 1, t), hi_own, lo_own, off_dup.reshape(n // t, 1, t), hi_dup, lo_dup)


def spans(off, n_blocks):
    edges = jnp.arange(n_blocks + 1, dtype=jnp.int32) * ROWS
    pos = jnp.sum((off[None, :] < edges[:, None]).astype(jnp.int32), axis=1)
    first = pos[:-1] // SEG_TILE
    count = jnp.where(pos[1:] > pos[:-1], (pos[1:] - 1) // SEG_TILE - first + 1, 0)
    return pos, first, count


def pick_at(one_hot, values):
    return jnp.sum(one_hot * values[None, :], axis=1)


def expand(count, length):
    end = jnp.cumsum(count)
    step = jnp.minimum(jnp.arange(length, dtype=jnp.int32), end[-1] - 1)
    begin = end - count
    in_block = jnp.logical_and(step[:, None] >= begin[None, :], step[:, None] < end[None, :]).astype(jnp.int32)
    return in_block, step - pick_at(in_block, begin), end[-1]


def take_rows(rows, idx):
    return rows.at[idx].get(mode='promise_in_bounds')


def solution(mesh):
    emb_size = mesh.shape['emb']
    dp_size = mesh.shape['dp']
    tok_spec = P(('dp', 'emb'))
    row_spec = P(('dp', 'emb'), None)
    tab_spec = P(None, 'emb', None)
    full_spec = P()

    def device_body(ids, x_loc, dy_loc, tabs, w_up, w_down, w_gate, w_proj):
        tok_dev = ids.shape[0]
        layers, rows_dev, dim = tabs.shape
        cap = 2 * tok_dev // emb_size
        n = emb_size * cap
        n_blocks = -(-rows_dev // ROWS)
        iota_tok = jnp.arange(tok_dev, dtype=jnp.int32)
        iota_n = jnp.arange(n, dtype=jnp.int32)

        ids_sorted, order = lax.sort((ids, iota_tok), num_keys=1)
        bounds = jnp.arange(emb_size + 1, dtype=jnp.int32) * rows_dev
        starts = jnp.sum((ids[None, :] < bounds[:, None]).astype(jnp.int32), axis=1)
        ids_pad = jnp.concatenate([ids_sorted, jnp.full((cap,), DEAD, jnp.int32)])
        order_pad = jnp.concatenate([order, jnp.zeros((cap,), jnp.int32)])
        slot_id = jnp.stack([lax.dynamic_slice(ids_pad, (starts[o],), (cap,)) for o in range(emb_size)])
        slot_src = jnp.concatenate([lax.dynamic_slice(order_pad, (starts[o],), (cap,)) for o in range(emb_size)])
        rank = jnp.arange(cap, dtype=jnp.int32)[None, :]
        alive = rank < (starts[1:] - starts[:-1])[:, None]
        send_off = jnp.where(alive, slot_id - bounds[:-1, None], DEAD)
        recv_off = lax.all_to_all(send_off, 'emb', 0, 0, tiled=True).reshape(n)

        def exchange(rows):
            return lax.all_to_all(rows.reshape(emb_size, cap, dim), 'emb', 0, 0, tiled=True).reshape(n, dim)

        off_own, order_own = lax.sort((recv_off, iota_n), num_keys=1)
        swap = [(i, dp_size - 1 - i) for i in range(dp_size)]
        off_dup = lax.ppermute(off_own, 'dp', swap)

        def lookup(off):
            live = jnp.sum((off < DEAD).astype(jnp.int32)).reshape(1)
            tiles = jnp.maximum((live + TILE - 1) // TILE, 1)
            pos, first, count = spans(off, n_blocks)
            hot, inner, pairs = expand(count, n // SEG_TILE + n_blocks)
            tile = pick_at(hot, first) + inner
            blk = pick_at(hot, jnp.arange(n_blocks, dtype=jnp.int32))
            used = (live[0] + SEG_TILE - 1) // SEG_TILE
            extra = tiles[0] * (TILE // SEG_TILE) - used
            past = jnp.minimum(jnp.arange(tile.shape[0], dtype=jnp.int32) - pairs, extra - 1)
            tile = jnp.where(past < 0, tile, used + past)
            tile = jnp.clip(tile, 0, n // SEG_TILE - 1)
            return run_pick(pairs + extra, tile, blk, off, tabs), live, tiles, (pos, first, count)

        x_recv = exchange(take_rows(x_loc, slot_src))
        d_send = take_rows(dy_loc, slot_src)
        e_own, live_own, tiles_own, (pos_o, first_o, count_o) = lookup(off_own)
        e_dup, live_dup, tiles_dup, (pos_d, first_d, count_d) = lookup(off_dup)
        d_send, e_own, e_dup = lax.optimization_barrier((d_send, e_own, e_dup))
        x_recv, e_own, e_dup = lax.optimization_barrier((x_recv, e_own, e_dup))
        d_recv = exchange(d_send)
        x_own = take_rows(x_recv, order_own)
        d_own = take_rows(d_recv, order_own)
        x_dup = lax.ppermute(x_own, 'dp', swap)
        d_dup = lax.ppermute(d_own, 'dp', swap)
        weights = (w_up, w_down, w_gate, w_proj)

        def batch(last, e, live, tiles, x, d):
            xl, du, dg, a, *fin = run_forward(last, tiles, x, e, *weights)
            return *run_backward(tiles, live, d, xl, du, dg, a, e, *weights), *fin

        hi_own, lo_own, x_fin = batch(True, e_own, live_own, tiles_own, x_own, d_own)
        x_dup, hi_own, lo_own = lax.optimization_barrier((x_dup, hi_own, lo_own))
        hi_dup, lo_dup = batch(False, e_dup, live_dup, tiles_dup, x_dup, d_dup)

        _, back = lax.sort((order_own, iota_n), num_keys=1)
        _, place = lax.sort((order, iota_tok), num_keys=1)
        x_fin, hi_dup, lo_dup = lax.optimization_barrier((x_fin, hi_dup, lo_dup))
        returned = exchange(take_rows(x_fin, back))
        owner_hot = (ids[:, None] // rows_dev == jnp.arange(emb_size, dtype=jnp.int32)[None, :]).astype(jnp.int32)
        slot = place + pick_at(owner_hot, jnp.arange(emb_size, dtype=jnp.int32) * cap - starts[:-1])

        per_block = jnp.maximum(count_o + count_d, 1)
        hot, inner, steps = expand(per_block, 2 * (n // SEG_TILE + n_blocks))
        n_own = pick_at(hot, count_o)
        sel = (inner >= n_own).astype(jnp.int32)
        top = n // SEG_TILE - 1
        t_own = jnp.clip(pick_at(hot, first_o) + jnp.minimum(inner, jnp.maximum(n_own - 1, 0)), 0, top)
        t_dup = jnp.clip(pick_at(hot, first_d) + jnp.maximum(inner - n_own, 0), 0, top)
        blk = pick_at(hot, jnp.arange(n_blocks, dtype=jnp.int32))
        d_tabs = run_sum(rows_dev, steps, (blk, t_own, t_dup, sel, pos_o, pos_d), off_own, hi_own, lo_own, off_dup, hi_dup, lo_dup)
        returned, d_tabs = lax.optimization_barrier((returned, d_tabs))
        return take_rows(returned, slot), d_tabs

    return jax.shard_map(device_body, mesh=mesh, in_specs=(tok_spec, row_spec, row_spec, tab_spec, full_spec, full_spec, full_spec, full_spec), out_specs=(row_spec, tab_spec), check_vma=False)
```

time: 4280 us -> 1810 us (0.42)
  Pallas kernels: 0 us -> 1300 us
  waiting for transfers between devices: 1150 us -> 2.03 us
  blocking collectives: 1140 us -> 0 us
  matrix products: 748 us -> 0 us
  other arithmetic: 652 us -> 35.2 us
  local copies, waits for them, and re-layouts: 548 us -> 241 us
  starting transfers between devices: 27.9 us -> 182 us
    pallas_call x0 -> x7, Pallas kernels: none -> 1300 us  [the longest x2 592 us: run_forward(): pl.pallas_call(functools.partial(forward_kernel, last), out_shape=[o[0] f...]
    all_to_all x4 -> x0, blocking collectives: 1130 us -> none  [device_body(): got_grad = lax.all_to_all(send_grad, 'emb', 0, 0, tiled=True)]
    all_gather x4 -> x0, waiting for transfers between devices: 1040 us -> none  [device_body(): all_grad = lax.all_gather(got_grad, 'dp', axis=0, tiled=True)]
    dot_general x29 -> x0, matrix products: 748 us -> none  [the longest x3 172 us: layer_backward(): jnp.einsum('td,fd->tf', d_next, w_down, preferred_element_type=jnp.float32)]
    scatter-add x4 -> x0, other arithmetic: 475 us -> none  [device_body(): jax.ops.segment_sum(all_grad, all_off, num_segments=rows_dev)]
    gather x12 -> x6, local copies, waits for them, and re-layouts: 446 us -> 236 us  [take_rows(): return rows.at[idx].get(mode='promise_in_bounds')]
    all_to_all x5 -> x4, starting transfers between devices: 27.7 us -> 180 us  [the longest x3 175 us: exchange(): lax.all_to_all(rows.reshape(emb_size, cap, dim), 'emb', 0, 0, tiled=True)]
    all_to_all x5 -> x4, waiting for transfers between devices: 111 us -> 2.02 us  [the longest x3 2.02 us: exchange(): lax.all_to_all(rows.reshape(emb_size, cap, dim), 'emb', 0, 0, tiled=True)]
  transfers between devices with their start and end apart: 9 -> 7, of which waited for: 7 -> 1; matrix products, arithmetic and copies ran while one was open for 21% -> 11% of each run, Pallas kernels for 0% -> 61%
where the time goes in v1:
time: 1810 us; the launch traced here: 1780 us
  Pallas kernels  1300 us (72%)
  local copies, waits for them, and re-layouts  241 us (13%)
  starting transfers between devices  182 us (10%)
  other arithmetic  35.2 us (2%)
  between operations  22 us (1%)
    pallas_call x2, Pallas kernels, run_forward(): pl.pallas_call(functools.partial(forward_kernel, last), out_shape=[o[0] f...  592 us
    pallas_call x2, Pallas kernels, run_backward(): pl.pallas_call(backward_kernel, out_shape=[jax.ShapeDtypeStruct((layers,...  475 us
    gather x6, local copies, waits for them, and re-layouts, take_rows(): return rows.at[idx].get(mode='promise_in_bounds')  236 us
    all_to_all x3, starting transfers between devices, exchange(): lax.all_to_all(rows.reshape(emb_size, cap, dim), 'emb', 0, 0, tiled=True)  175 us
    pallas_call x1, Pallas kernels, run_sum(): pl.pallas_call(sum_kernel, out_shape=jax.ShapeDtypeStruct((layers, rows_d...  127 us
    pallas_call x2, Pallas kernels, run_pick(): pl.pallas_call(functools.partial(pick_kernel, rows_dev), out_shape=jax.Sh...  101 us
  transfers between devices with their start and end apart: 7, of which 1 were waited for; matrix products, arithmetic and copies ran while one was open for 11% of the time, Pallas kernels for 61%

profile of v1, /device:TPU:0, one launch (start us, length us, event | category | flops | bytes accessed | tf_op | source)
XLA Modules:
  0.0 1777.8 jit_solution(17304616191305004366)
XLA Ops:
  12.9 5.9 sort.60
  24.8 5.5 all-to-all-start
  30.5 40.6 %gather_fusion = bf16[8192,768]{1,0:T(8,128)(2,1)} fusion(bf16[4096,768]{1,0:T(8,128)(2,1)} %param.9, s32[8192]{0:T(1024)S(1)} %broadcast_clamp_fusion), kind=kCustom, calls=%fused_computation | custom fusion | bytes 25198592 | tf_op jit(solution)/shard_map/gather | solution.py:387
  71.1 5.5 all-to-all-start.1
  76.7 40.7 %gather_fusion.1 = bf16[8192,768]{1,0:T(8,128)(2,1)} fusion(bf16[4096,768]{1,0:T(8,128)(2,1)} %param.10, s32[8192]{0:T(1024)S(1)} %broadcast_clamp_fusion), kind=kCustom, calls=%fused_computation.1 | custom fusion | bytes 25198592 | tf_op jit(solution)/shard_map/gather | solution.py:387
  117.4 6.2 sort.61
  123.6 1.6 collective-permute-start
  125.2 6.8 sort.62
  145.4 47.6 %pick.3.e_ref.refs_5_ = bf16[4,8192,768]{2,1,0:T(8,128)(2,1)} custom-call(s32[1]{0:T(128)} %bitcast.38.num_ref, s32[57]{0:T(128)} %fusion.5.refs_0_, s32[57]{0:T(128)} %get-tuple-element.73.refs_1_, s32[32,1,256]{2,1,0:T(1,128)} %bitcast.54, bf16[4,6288,768]{2,1,0:T(8,128)(2,1)} %refs_3_.3), custom_call_target="tpu_custom_call" | custom-call | flops 40000000000 | bytes 100663296 | tf_op jit(solution)/shard_map/pick/pallas_call | solution.py:292
  193.0 53.4 %pick.2.e_ref.refs_5_ = bf16[4,8192,768]{2,1,0:T(8,128)(2,1)} custom-call(s32[1]{0:T(128)} %bitcast.32.num_ref, s32[57]{0:T(128)} %fusion.4.refs_0_, s32[57]{0:T(128)} %get-tuple-element.119.refs_1_, s32[32,1,256]{2,1,0:T(1,128)} %bitcast.52, bf16[4,6288,768]{2,1,0:T(8,128)(2,1)} %refs_3_.3), custom_call_target="tpu_custom_call" | custom-call | flops 40000000000 | bytes 100663296 | tf_op jit(solution)/shard_map/pick/pallas_call | solution.py:292
  246.4 8.2 all-to-all-start.2
  254.7 43.3 %gather_fusion.2 = bf16[8192,768]{1,0:T(8,128)(2,1)} fusion(bf16[8192,768]{1,0:T(8,128)(2,1)} %bitcast.28, s32[8192]{0:T(1024)S(1)} %fusion), kind=kCustom, calls=%fused_computation.2 | custom fusion | bytes 25198592 | tf_op jit(solution)/shard_map/gather | solution.py:387
  298.4 328.9 %fwd.2 = (bf16[3,8192,768]{2,1,0:T(8,128)(2,1)}, f32[3,8192,3072]{2,1,0:T(8,128)}, f32[3,8192,768]{2,1,0:T(8,128)}, bf16[4,8192,768]{2,1,0:T(8,128)(2,1)}, bf16[8192,768]{1,0:T(8,128)(2,1)}) custom-call(s32[1]{0:T(128)S(6)} %max.31.nt_ref, bf16[8192,768]{1,0:T(8,128)(2,1)} %gather_fusion.2, bf16[4,8192,768]{2,1,0:T(8,128)(2,1)} %pick.2.e_ref.refs_5_, ...), custom_call_target="tpu_custom_call" | custom-call | flops 193273528320 | bytes 402653184 | tf_op jit(solution)/shard_map/fwd/pallas_call | solution.py:205
  627.3 43.2 %gather_fusion.3 = bf16[8192,768]{1,0:T(8,128)(2,1)} fusion(bf16[8192,768]{1,0:T(8,128)(2,1)} %bitcast.41, s32[8192]{0:T(1024)S(1)} %copy-done.3), kind=kCustom, calls=%fused_computation.3 | custom fusion | bytes 25198592 | tf_op jit(solution)/shard_map/gather | solution.py:387
  670.6 259.2 %bwd.2 = (bf16[4,8192,768]{2,1,0:T(8,128)(2,1)}, bf16[4,8192,768]{2,1,0:T(8,128)(2,1)}) custom-call(s32[1]{0:T(128)S(6)} %max.31.nt_ref, s32[1]{0:T(128)} %bitcast.17.n_ref, bf16[8192,768]{1,0:T(8,128)(2,1)} %gather_fusion.3, bf16[3,8192,768]{2,1,0:T(8,128)(2,1)} %get-tuple-element.45.refs_1_, f32[3,8192,3072]{2,1,0:T(8,128)} %get-tuple-element.46.refs_2_, ...), custom_call_target="tpu_custom_call" | custom-call | flops 193273528320 | bytes 402653184 | tf_op jit(solution)/shard_map/bwd/pallas_call | solution.py:240
  929.8 263.4 %fwd.3 = (bf16[3,8192,768]{2,1,0:T(8,128)(2,1)}, f32[3,8192,3072]{2,1,0:T(8,128)}, f32[3,8192,768]{2,1,0:T(8,128)}, bf16[4,8192,768]{2,1,0:T(8,128)(2,1)}) custom-call(s32[1]{0:T(128)S(6)} %max.33.nt_ref, bf16[8192,768]{1,0:T(8,128)(2,1)} %collective-permute-done.2.x_ref, bf16[4,8192,768]{2,1,0:T(8,128)(2,1)} %pick.3.e_ref.refs_5_, ...), custom_call_target="tpu_custom_call" | custom-call | flops 193273528320 | bytes 402653184 | tf_op jit(solution)/shard_map/fwd/pallas_call | solution.py:205
  1193.2 216.0 %bwd.3 = (bf16[4,8192,768]{2,1,0:T(8,128)(2,1)}, bf16[4,8192,768]{2,1,0:T(8,128)(2,1)}) custom-call(s32[1]{0:T(128)S(6)} %max.33.nt_ref, s32[1]{0:T(128)} %bitcast.36.n_ref, bf16[8192,768]{1,0:T(8,128)(2,1)} %collective-permute-done.1.refs_0_, bf16[3,8192,768]{2,1,0:T(8,128)(2,1)} %get-tuple-element.53.refs_1_, f32[3,8192,3072]{2,1,0:T(8,128)} %get-tuple-element.54.refs_2_, ...), custom_call_target="tpu_custom_call" | custom-call | flops 193273528320 | bytes 402653184 | tf_op jit(solution)/shard_map/bwd/pallas_call | solution.py:240
  1409.2 43.3 %gather_fusion.4 = bf16[8192,768]{1,0:T(8,128)(2,1)} fusion(bf16[8192,768]{1,0:T(8,128)(2,1)} %get-tuple-element.59, s32[8192]{0:T(1024)S(1)} %copy-done.5), kind=kCustom, calls=%fused_computation.4 | custom fusion | bytes 25198592 | tf_op jit(solution)/shard_map/gather | solution.py:387
  1452.5 160.8 %all-to-all-start.3 = ((bf16[8,1024,768]{2,1,0:T(8,128)(2,1)}), bf16[8,1024,768]{2,1,0:T(8,128)(2,1)}, u32[]{:S(2)}, u32[]{:S(2)}) async-start(bf16[8,1024,768]{2,1,0:T(8,128)(2,1)} %bitcast.51), calls=%async_computation.3 | async-start | bytes 25165824 | tf_op jit(solution)/shard_map/all_to_all | solution.py:420
  1613.3 5.8 sort.63
  1619.2 1.3 slice.108
  1623.0 127.3 %tabsum.1 = f32[4,6288,768]{2,1,0:T(8,128)} custom-call(s32[1]{0:T(128)} %bitcast.45.num_ref, s32[114]{0:T(128)} %get-tuple-element.72.refs_0_, s32[114]{0:T(128)} %get-tuple-element.103.refs_1_, s32[114]{0:T(128)} %get-tuple-element.102.refs_2_, s32[114]{0:T(128)} %compare_convert_fusion.refs_3_, s32[26]{0:T(128)} %copy-done.12, s32[26]{0:T(128)} %copy-done.11, ...), custom_call_target="tpu_custom_call" | custom-call | flops 60000002048 | bytes 278593536 | tf_op jit(solution)/shard_map/tabsum/pallas_call | solution.py:352
  1750.3 2.0 all-to-all-done.3
  1752.3 25.2 %gather_fusion.5 = bf16[4096,768]{1,0:T(8,128)(2,1)} fusion(bf16[8192,768]{1,0:T(8,128)(2,1)} %bitcast.43, s32[4096]{0:T(1024)S(1)} %fusion.2), kind=kCustom, calls=%fused_computation.5 | custom fusion | bytes 12599296 | tf_op jit(solution)/shard_map/gather | solution.py:387
  (110 shorter events, 14.1 us)
Async XLA Ops:
  18.8 11.7 copy-start.6
  24.8 46.4 %all-to-all-start = ((s32[8,1,1024]{2,1,0:T(1,128)}), s32[8,1,1024]{2,1,0:T(1,128)S(1)}, u32[]{:S(2)}, u32[]{:S(2)}) async-start(s32[8,1,1024]{2,1,0:T(1,128)} %compare_select_fusion.1), calls=%async_computation | async-start | bytes 65536 | tf_op jit(solution)/shard_map/all_to_all | solution.py:417
  71.1 175.3 %all-to-all-start.1 = ((bf16[8,1024,768]{2,1,0:T(8,128)(2,1)}), bf16[8,1024,768]{2,1,0:T(8,128)(2,1)}, u32[]{:S(2)}, u32[]{:S(2)}) async-start(bf16[8,1024,768]{2,1,0:T(8,128)(2,1)} %bitcast.50), calls=%async_computation.1 | async-start | bytes 25165824 | tf_op jit(solution)/shard_map/all_to_all | solution.py:420
  123.6 69.4 %copy-start = (s32[8192]{0:T(1024)}, s32[8192]{0:T(1024)S(1)}, u32[]{:S(2)}) copy-start(s32[8192]{0:T(1024)S(1)} %get-tuple-element.36) | copy-start | bytes 98308
  123.6 11.0 collective-permute-start
  132.0 122.7 %copy-start.2 = (s32[8192]{0:T(1024)}, s32[8192]{0:T(1024)S(1)}, u32[]{:S(2)}) copy-start(s32[8192]{0:T(1024)S(1)} %fusion) | copy-start | bytes 98308
  134.6 10.8 copy-start.1
  136.9 5.6 copy-start.11
  136.9 5.6 copy-start.12
  137.0 6.1 copy-start.15
  246.4 380.9 %all-to-all-start.2 = ((bf16[8,1024,768]{2,1,0:T(8,128)(2,1)}), bf16[8,1024,768]{2,1,0:T(8,128)(2,1)}, u32[]{:S(2)}, u32[]{:S(2)}) async-start(bf16[8,1024,768]{2,1,0:T(8,128)(2,1)} %bitcast.49), calls=%async_computation.2 | async-start | bytes 25165824 | tf_op jit(solution)/shard_map/all_to_all | solution.py:420
  298.0 631.8 %collective-permute-start.2 = (bf16[8192,768]{1,0:T(8,128)(2,1)}, bf16[8192,768]{1,0:T(8,128)(2,1)}, u32[]{:S(2)}, u32[]{:S(2)}) collective-permute-start(bf16[8192,768]{1,0:T(8,128)(2,1)} %gather_fusion.2), channel_id=1, source_target_pairs={{0,8},{8,0},{1,9},{9,1},{2,10},{10,2},{3,11},{11,3},{4,12},{12,4},... | collective-permute-start | bytes 37748744 | tf_op jit(solution)/shard_map/ppermute | solution.py:449
  298.4 328.9 %copy-start.3 = (s32[8192]{0:T(1024)S(1)}, s32[8192]{0:T(1024)}, u32[]{:S(2)}) copy-start(s32[8192]{0:T(1024)} %copy-done.2) | copy-start | bytes 98308
  670.6 522.6 %collective-permute-start.1 = (bf16[8192,768]{1,0:T(8,128)(2,1)}, bf16[8192,768]{1,0:T(8,128)(2,1)}, u32[]{:S(2)}, u32[]{:S(2)}) collective-permute-start(bf16[8192,768]{1,0:T(8,128)(2,1)} %gather_fusion.3), channel_id=1, source_target_pairs={{0,8},{8,0},{1,9},{9,1},{2,10},{10,2},{3,11},{11,3},{4,12},{12,4},... | collective-permute-start | bytes 37748744 | tf_op jit(solution)/shard_map/ppermute | solution.py:450
  1193.2 216.0 %copy-start.5 = (s32[8192]{0:T(1024)S(1)}, s32[8192]{0:T(1024)}, u32[]{:S(2)}) copy-start(s32[8192]{0:T(1024)} %fusion.1) | copy-start | bytes 98308
  1452.4 160.9 %copy-start.7 = (s32[4096]{0:T(1024)S(1)}, s32[4096]{0:T(1024)}, u32[]{:S(2)}) copy-start(s32[4096]{0:T(1024)} %copy-done.6) | copy-start | bytes 49156
  1452.4 166.6 %copy-start.4 = (s32[4096]{0:T(1024)S(1)}, s32[4096]{0:T(1024)}, u32[]{:S(2)}) copy-start(s32[4096]{0:T(1024)} %param.8) | copy-start | bytes 49156
  1452.5 166.7 %copy-start.19 = (s32[8]{0:T(128)S(1)}, s32[8]{0:T(128)}, u32[]{:S(2)}) copy-start(s32[8]{0:T(128)} %get-tuple-element.104) | copy-start | bytes 100
  1452.5 168.8 %copy-start.10 = (s32[25]{0:T(128)S(1)}, s32[25]{0:T(128)}, u32[]{:S(2)}) copy-start(s32[25]{0:T(128)} %copy-done.9) | copy-start | bytes 304
  1452.5 168.8 %copy-start.14 = (s32[25]{0:T(128)S(1)}, s32[25]{0:T(128)}, u32[]{:S(2)}) copy-start(s32[25]{0:T(128)} %copy-done.13) | copy-start | bytes 304
  1452.5 168.8 %copy-start.16 = (s32[25]{0:T(128)S(1)}, s32[25]{0:T(128)}, u32[]{:S(2)}) copy-start(s32[25]{0:T(128)} %copy-done.15) | copy-start | bytes 304
  1452.5 168.8 %copy-start.18 = (s32[25]{0:T(128)S(1)}, s32[25]{0:T(128)}, u32[]{:S(2)}) copy-start(s32[25]{0:T(128)} %copy-done.17) | copy-start | bytes 304
  1452.5 168.8 %copy-start.20 = (s32[25]{0:T(128)S(1)}, s32[25]{0:T(128)}, u32[]{:S(2)}) copy-start(s32[25]{0:T(128)} %get-tuple-element.106) | copy-start | bytes 304
  1452.5 299.8 %all-to-all-start.3 = ((bf16[8,1024,768]{2,1,0:T(8,128)(2,1)}), bf16[8,1024,768]{2,1,0:T(8,128)(2,1)}, u32[]{:S(2)}, u32[]{:S(2)}) async-start(bf16[8,1024,768]{2,1,0:T(8,128)(2,1)} %bitcast.51), calls=%async_computation.3 | async-start | bytes 25165824 | tf_op jit(solution)/shard_map/all_to_all | solution.py:420
  (4 other events, 12.3 us)
